TPU v7x, 256 devices: a whole 4x4x8 slice. The times are simulated.
256 devices in a mesh: px: 16 (over x_hi, z), py: 16 (over y, x_lo, core).
Axes of the slice: x: 4 (x_hi: 2, x_lo: 2; x = x_hi * 2 + x_lo), y: 4, z: 8, core: 2. Of those that a mesh axis runs over, the one named last changes fastest.
Arguments:
- particles: float32 [256, 2, 2, 128, 128], P(('px', 'py')), may hold values from -11 to 11
- orientation: int32 [256], P(('px', 'py')), may hold values from 0 to 7
- wedge_index: int32 [256], P(('px', 'py')), may hold values from 0 to 3
- half_set: int32 [256], P(('px', 'py')), may hold values from 0 to 1
- shell_map: int32 [2, 256, 256], P(None, ('px', 'py')), may hold values from 0 to 31, as said below
Outputs:
- half_maps: float32 [2, 2, 2, 256, 256], P(None, None, None, ('px', 'py'))
- fsc: float32 [32], replicated
Inputs may be any that keep to these rules, and one draw needn't show every extreme that they name: `shell_map`: every shell number occurs in every draw.
All inputs are finite; a program needn't handle non-finite values.
Results may differ from a plain program's by a relative error of at most 0.0003.
Values sent between devices are 32-bit elements; how exact they have to be, the bound alone decides.
A program may use at most 64 MiB of HBM per device.

v0:
```python
import math

import jax
import jax.numpy as jnp
from jax import lax
from jax.sharding import Mesh
from jax.sharding import PartitionSpec as P

NSHELL = 32
PX_PY = ("px_0", "px_1", "py_0", "py_1", "py_2")
PX = ("px_0", "px_1")
PY = ("py_0", "py_1", "py_2")


wedge_rise = (1, 3, 2, 3)
wedge_run = (1, 2, 1, 1)
sign_first = (1.0, -1.0, -1.0, 1.0, 1.0, -1.0, -1.0, 1.0)
sign_second = (1.0, 1.0, -1.0, -1.0, -1.0, -1.0, 1.0, 1.0)
highest = lax.Precision.HIGHEST


def cut_along(value, dim, size):
    before, after = (value.shape[:dim], value.shape[dim + 1 :])
    return jnp.moveaxis(value.reshape(*before, size, -1, *after), dim, 0)


def scatter_pairs(value, chips, core, dim):
    sizes = (lax.axis_size(chips), lax.axis_size(core))
    tiles = cut_along(value, dim, sizes[0] * sizes[1])
    inside = tiles.shape[1:]
    tiles = tiles.reshape(*sizes, *inside).swapaxes(0, 1).reshape(-1, *inside)
    tiles = lax.psum_scatter(tiles, core, scatter_dimension=0, tiled=True)
    return lax.psum_scatter(tiles, chips, scatter_dimension=0, tiled=True)[0]


def over_axes(value, axes):
    for axis in axes:
        value = lax.psum(value, axis)
    return value


def select(lookup, position):
    entries = jnp.array(lookup)
    return jnp.sum(jnp.where(jnp.arange(len(lookup)) == position, entries, jnp.zeros_like(entries)))


def angle_table(sources, targets, extent):
    phases = sources[:, None] * targets[None, :] % extent
    angles = phases.astype(jnp.float32) * (2.0 * math.pi / extent)
    factor = 1.0 / math.sqrt(extent)
    return (jnp.cos(angles) * factor, jnp.sin(angles) * factor)


def coverage(plane_abs, spectral_abs, wedge_id):
    rise_value = select(wedge_rise, wedge_id)
    run_value = select(wedge_run, wedge_id)
    return (plane_abs[:, None] * run_value <= spectral_abs[None, :] * rise_value).astype(
        jnp.float32
    )


def shards(particles, orientation, wedge_index, half_set, shell_map):
    planes = particles.shape[2]
    box_side = particles.shape[3]
    extent = shell_map.shape[2]
    own_rows = shell_map.shape[1]
    plane_abs = jnp.abs((jnp.arange(planes, dtype=jnp.int32) - planes // 2) * (extent // planes))
    spectral = jnp.arange(extent, dtype=jnp.int32)
    spectral_abs = jnp.minimum(spectral, extent - spectral)
    cos_fwd, sin_fwd = angle_table(
        jnp.arange(box_side, dtype=jnp.int32) - box_side // 2, spectral, extent
    )
    totals = jnp.zeros((2, 2, planes, extent, extent), jnp.float32)
    cover_sum = jnp.zeros((2, planes, extent, extent), jnp.float32)
    source = particles[0]
    turn_index = orientation[0]
    swapped = turn_index % 2 == 1
    source = jnp.where(turn_index >= 4, jnp.roll(jnp.flip(source, 1), 1, 1), source)
    source = jnp.where(swapped, jnp.swapaxes(source, 2, 3), source)
    sign_outer = select(sign_first, turn_index)
    sign_inner = select(sign_second, turn_index)
    along_cos = jnp.einsum("czab,bk->czak", source, cos_fwd, precision=highest)
    along_sin = jnp.einsum("czab,bk->czak", source, sin_fwd, precision=highest)
    partial_turn = jnp.stack(
        [along_cos[0] + sign_inner * along_sin[1], along_cos[1] - sign_inner * along_sin[0]]
    )
    outer_cos = jnp.einsum("czak,aj->czjk", partial_turn, cos_fwd, precision=highest)
    outer_sin = jnp.einsum("czak,aj->czjk", partial_turn, sin_fwd, precision=highest)
    spectrum = jnp.stack(
        [outer_cos[0] + sign_outer * outer_sin[1], outer_cos[1] - sign_outer * outer_sin[0]]
    )
    covered = coverage(plane_abs, spectral_abs, wedge_index[0])
    covered = jnp.where(swapped, covered[:, None, :], covered[:, :, None])
    half_id = half_set[0]
    current = lax.dynamic_index_in_dim(totals, half_id, 0, False)
    totals = lax.dynamic_update_index_in_dim(totals, current + spectrum * covered, half_id, 0)
    present = lax.dynamic_index_in_dim(cover_sum, half_id, 0, False)
    cover_sum = lax.dynamic_update_index_in_dim(cover_sum, present + covered, half_id, 0)
    reduced, cover = (
        scatter_pairs(totals, ("px_0", "px_1", "py_0", "py_1"), "py_2", 3),
        scatter_pairs(cover_sum, ("px_0", "px_1", "py_0", "py_1"), "py_2", 2),
    )
    average = reduced / jnp.maximum(cover, 1.0)[:, None]
    cross = average[0, 0] * average[1, 0] + average[0, 1] * average[1, 1]
    power_first = average[0, 0] * average[0, 0] + average[0, 1] * average[0, 1]
    power_second = average[1, 0] * average[1, 0] + average[1, 1] * average[1, 1]
    stacked = jnp.stack([cross, power_first, power_second]).reshape(3, -1)
    membership = (shell_map.reshape(-1)[:, None] == jnp.arange(NSHELL)).astype(jnp.float32)
    shell_part = jnp.dot(stacked, membership, precision=highest)
    shell_total = over_axes(shell_part, PX_PY)
    fsc = shell_total[0] / (jnp.sqrt(shell_total[1] * shell_total[2]) + 1e-06)
    n_rows = lax.axis_size(PX)
    n_columns = lax.axis_size(PY)
    cos_y, sin_y = angle_table(spectral, spectral, extent)
    middle_cos = jnp.einsum("hcztk,kp->hczpt", average, cos_y, precision=highest)
    middle_sin = jnp.einsum("hcztk,kp->hczpt", average, sin_y, precision=highest)
    middle = jnp.stack(
        [middle_cos[:, 0] - middle_sin[:, 1], middle_sin[:, 0] + middle_cos[:, 1]], axis=1
    )
    arrived = lax.all_to_all(
        lax.all_to_all(middle, PX, split_axis=3, concat_axis=4, tiled=True),
        PY,
        split_axis=3,
        concat_axis=4,
        tiled=True,
    )
    x_slot = spectral // own_rows
    x_source = (x_slot % n_rows * n_columns + x_slot // n_rows) * own_rows + spectral % own_rows
    cos_x, sin_x = angle_table(x_source, spectral, extent)
    final_cos = jnp.einsum("hczym,mx->hczyx", arrived, cos_x, precision=highest)
    final_sin = jnp.einsum("hczym,mx->hczyx", arrived, sin_x, precision=highest)
    half_maps = jnp.stack(
        [final_cos[:, 0] - final_sin[:, 1], final_sin[:, 0] + final_cos[:, 1]], axis=1
    )
    return (half_maps, fsc)


def solution(mesh):
    torus = Mesh(mesh.devices.reshape(2, 8, 4, 2, 2), ("px_0", "px_1", "py_0", "py_1", "py_2"))
    in_specs = (
        P(PX_PY, None, None, None, None),
        P(PX_PY),
        P(PX_PY),
        P(PX_PY),
        P(None, PX_PY, None),
    )
    out_specs = (P(None, None, None, PX_PY, None), P())
    return jax.shard_map(
        shards, mesh=torus, in_specs=in_specs, out_specs=out_specs, check_vma=False
    )
```

profile of v0, /device:TPU:1, one launch (start us, length us, event | category | flops | bytes accessed | tf_op | source)
XLA Modules:
  0.0 362.2 jit_solution(7222236951428507306)
XLA Ops:
  8.5 1.4 fusion.73
  12.8 1.3 copy.58
  15.2 1.1 fusion.34
  16.3 1.1 fusion.38
  18.1 1.5 convolution_bitcast_fusion.1
  19.5 1.5 convolution_bitcast_fusion
  21.0 0.8 fusion.3
  22.5 0.9 copy_dynamic-update-slice_fusion
  23.4 2.6 copy.55
  26.2 6.3 %reduce-scatter.5.cloned.1.call-done = f32[128,2,2,1,256]{4,0,2,1,3:T(8,128)} async-done(((f32[256,2,2,1,256]{4,0,2,1,3:T(8,128)}), f32[128,2,2,1,256]{4,0,2,1,3:T(8,128)}) %reduce-scatter.5.cloned.1.call-update) | async-done | bytes 524304 | tf_op jit(solution)/shard_map/reduce_scatter | solution.py:32
  32.5 2.2 copy.59
  34.8 16.2 %reduce-scatter.3.cloned.1.call-done = f32[128,2,2,2,1,256]{5,0,3,2,1,4:T(8,128)} async-done(((f32[256,2,2,2,1,256]{5,0,3,2,1,4:T(8,128)}), f32[128,2,2,2,1,256]{5,0,3,2,1,4:T(8,128)}) %reduce-scatter.3.cloned.1.call-update) | async-done | bytes 1048592 | tf_op jit(solution)/shard_map/reduce_scatter | solution.py:32
  51.0 3.0 copy.56
  54.7 224.0 %all-reduce.5.cloned.1.call-done = (f32[128,2,2,2,1,256]{5,3,4,2,1,0:T(2,128)}, f32[128,2,2,1,256]{4,2,3,1,0:T(2,128)}) async-done(((f32[128,2,2,2,1,256]{5,3,4,2,1,0:T(2,128)}, f32[128,2,2,1,256]{4,2,3,1,0:T(2,128)}), (f32[128,2,2,2,1,256]{5,3,4,2,1,0:T(2,128)}, f32[128,2,2,1,256]{4,2,3,1,0:T(2,128)})) %all-reduce.5.cloned.1.call-update) | async-done | bytes 1572880
  278.7 1.3 fusion.65
  280.0 1.3 bitcast_divide_fusion
  281.4 1.4 bitcast_divide_fusion.1
  282.7 1.3 convolution_bitcast_fusion.4
  284.0 1.2 convolution_bitcast_fusion.5
  285.7 1.3 reshape.364
  286.9 5.9 %all-to-all-start = ((f32[16,1,128]{2,1,0:T(1,128)}), f32[16,1,128]{2,1,0:T(1,128)S(1)}, u32[]{:S(2)}, u32[]{:S(2)}) async-start(f32[16,1,128]{2,1,0:T(1,128)} %reshape.364), calls=%async_computation.2 | async-start | bytes 16384 | tf_op jit(solution)/shard_map/all_to_all | solution.py:121
  293.2 5.3 %psum.35 = f32[3,32]{1,0:T(4,128)S(1)} all-reduce(f32[3,32]{1,0:T(4,128)S(1)} %fusion.30), channel_id=1, replica_groups=mesh['px_0'=2,'px_1'=8,'py_0'=4,'py_1'=2,'py_2'=2] {'px_0'}, use_global_device_ids=true, to_apply=%region_8.9 | all-reduce | flops 96 | bytes 768 | tf_op jit(solution)/shard_map/psum | solution.py:38
  298.5 13.8 %psum.36 = f32[3,32]{1,0:T(4,128)S(1)} all-reduce(f32[3,32]{1,0:T(4,128)S(1)} %psum.35), channel_id=1, replica_groups=mesh['px_0'=2,'px_1'=8,'py_0'=4,'py_1'=2,'py_2'=2] {'px_1'}, use_global_device_ids=true, to_apply=%region_9.10 | all-reduce | flops 96 | bytes 768 | tf_op jit(solution)/shard_map/psum | solution.py:38
  312.3 7.6 %psum.37 = f32[3,32]{1,0:T(4,128)S(1)} all-reduce(f32[3,32]{1,0:T(4,128)S(1)} %psum.36), channel_id=1, replica_groups=mesh['px_0'=2,'px_1'=8,'py_0'=4,'py_1'=2,'py_2'=2] {'py_0'}, use_global_device_ids=true, to_apply=%region_10.11 | all-reduce | flops 96 | bytes 768 | tf_op jit(solution)/shard_map/psum | solution.py:38
  319.8 3.8 %psum.38 = f32[3,32]{1,0:T(4,128)S(1)} all-reduce(f32[3,32]{1,0:T(4,128)S(1)} %psum.37), channel_id=1, replica_groups=mesh['px_0'=2,'px_1'=8,'py_0'=4,'py_1'=2,'py_2'=2] {'py_1'}, use_global_device_ids=true, to_apply=%region_11.12 | all-reduce | flops 96 | bytes 768 | tf_op jit(solution)/shard_map/psum | solution.py:38
  323.6 15.4 %psum.39 = f32[3,32]{1,0:T(4,128)S(1)} all-reduce(f32[3,32]{1,0:T(4,128)S(1)} %psum.38), channel_id=1, replica_groups=mesh['px_0'=2,'px_1'=8,'py_0'=4,'py_1'=2,'py_2'=2] {'py_2'}, use_global_device_ids=true, to_apply=%region_12.13 | all-reduce | flops 96 | bytes 768 | tf_op jit(solution)/shard_map/psum | solution.py:38
  340.3 0.8 reshape.365
  341.6 0.7 reshape.366
  342.3 3.6 all-to-all-start.1
  346.5 5.0 %all-to-all-done.1 = f32[16,1,128]{2,1,0:T(1,128)S(1)} async-done(((f32[16,1,128]{2,1,0:T(1,128)}), f32[16,1,128]{2,1,0:T(1,128)S(1)}, u32[]{:S(2)}, u32[]{:S(2)}) %all-to-all-start.1) | async-done | bytes 8224 | tf_op jit(solution)/shard_map/all_to_all | solution.py:120
  352.4 1.3 convolution_bitcast_fusion.2
  353.7 1.3 convolution_bitcast_fusion.3
  (52 shorter events, 10.0 us)
Async XLA Ops:
  7.2 25.4 %reduce-scatter.5.cloned.1.call-start = ((), (), s32[]{:S(2)}) async-start(), calls=%async_computation.5 | async-start | bytes 1572864 | tf_op jit(solution)/shard_map/reduce_scatter | solution.py:32
  12.3 2.0 copy-start.1
  12.3 2.0 copy-start.2
  12.4 2.7 copy-start
  14.2 36.9 %reduce-scatter.3.cloned.1.call-start = ((), (), s32[]{:S(2)}) async-start(), calls=%async_computation.4 | async-start | bytes 3145728 | tf_op jit(solution)/shard_map/reduce_scatter | solution.py:32
  26.0 252.7 %all-reduce.5.cloned.1.call-start = ((), (), s32[]{:S(2)}) async-start(), calls=%async_computation.6 | async-start | bytes 3145728
  34.8 19.3 %copy-start.4 = (u32[256]{0:T(256)S(1)}, u32[256]{0:T(256)}, u32[]{:S(2)}) copy-start(u32[256]{0:T(256)} %constant.150) | copy-start | bytes 3076
  54.1 238.8 %copy-start.3 = (s32[2,1,256]{2,1,0:T(1,128)S(1)}, s32[2,1,256]{2,1,0:T(1,128)}, u32[]{:S(2)}) copy-start(s32[2,1,256]{2,1,0:T(1,128)} %param.13) | copy-start | bytes 6148
  286.9 52.1 %all-to-all-start = ((f32[16,1,128]{2,1,0:T(1,128)}), f32[16,1,128]{2,1,0:T(1,128)S(1)}, u32[]{:S(2)}, u32[]{:S(2)}) async-start(f32[16,1,128]{2,1,0:T(1,128)} %reshape.364), calls=%async_computation.2 | async-start | bytes 16384 | tf_op jit(solution)/shard_map/all_to_all | solution.py:121
  342.3 9.1 %all-to-all-start.1 = ((f32[16,1,128]{2,1,0:T(1,128)}), f32[16,1,128]{2,1,0:T(1,128)S(1)}, u32[]{:S(2)}, u32[]{:S(2)}) async-start(f32[16,1,128]{2,1,0:T(1,128)} %reshape.366), calls=%async_computation.3 | async-start | bytes 16384 | tf_op jit(solution)/shard_map/all_to_all | solution.py:120
Sparse Core Ops, SparseCore 0:
  14.3 18.2 reduce-scatter.4
  35.0 15.9 reduce-scatter.2
  56.5 222.1 all-reduce.4
where the time goes:
time: 363 us; the launch traced here: 362 us
  waiting for transfers between devices  252 us (69%)
  blocking collectives  45.8 us (13%)
  local copies, waits for them, and re-layouts  16.8 us (5%)
  between operations  16.1 us (4%)
  other arithmetic  11.7 us (3%)
  matrix products  10.4 us (3%)
  starting transfers between devices  9.85 us (3%)
    unnamed x4, waiting for transfers between devices  224 us
    psum x5, blocking collectives, over_axes(): value = lax.psum(value, axis)  45.8 us
    reduce_scatter x2, waiting for transfers between devices, scatter_pairs(): tiles = lax.psum_scatter(tiles, core, scatter_dimension=0, tiled=True)  22.6 us
  transfers between devices with their start and end apart: 5, of which 4 were waited for; matrix products, arithmetic and copies ran while one was open for 4% of the time, Pallas kernels for 0%

commit v1 on v0

v1 whole, which is shorter than its diff:
```python
import functools
import math

import jax
import jax.numpy as jnp
import numpy as np
from jax import lax
from jax.experimental import pallas as pl
from jax.experimental.pallas import tpu as pltpu
from jax.sharding import PartitionSpec as P

RISE = (1, 3, 2, 3)
RUN = (1, 2, 1, 1)
NSHELL = 32
SIDE = 16
EXTENT = 256
BOX = 128
KZ = 128
THRESHOLDS = tuple(-(-KZ * run // rise) for rise, run in zip(RISE, RUN))
MESH = pl.DeviceIdType.MESH
f32 = jnp.float32
bf16 = jnp.bfloat16
NT = (((1,), (1,)), ((), ()))
NN = (((1,), (0,)), ((), ()))
MAPLANE = 96


def halves(table):
    table = jnp.asarray(table, f32)
    upper = table.astype(bf16)
    lower = (table - upper.astype(f32)).astype(bf16)
    return jnp.stack([upper, lower])


def tables():
    freq = np.arange(EXTENT)
    cell = np.arange(BOX) - BOX // 2
    scale = 1.0 / math.sqrt(EXTENT)
    unit = 2.0 * math.pi / EXTENT
    rows = np.arange(SIDE)
    order = (rows[None, :] * SIDE + rows[:, None]).reshape(-1)
    angle = (order[:, None] * cell[None, :] % EXTENT) * unit
    first = np.concatenate([np.cos(angle), np.sin(angle)], 1) * scale
    angle = (cell[:, None] * freq[None, :] % EXTENT) * unit
    cosine, sine = np.cos(angle) * scale, np.sin(angle) * scale
    second = np.block([[cosine, -sine], [sine, cosine]])
    angle = (freq[:, None] * freq[None, :] % EXTENT) * unit
    back = np.concatenate([np.cos(angle), np.sin(angle)], 1) * scale
    return [np.asarray(t, np.float32) for t in (first, second, back)]


def cut(value):
    upper = value.astype(bf16)
    return upper, (value - upper.astype(f32)).astype(bf16)


def dot(a, b, dims):
    return lax.dot_general(a, b, dims, preferred_element_type=f32)


def dot3(a, b, dims):
    return dot(a[0], b[0], dims) + (dot(a[0], b[1], dims) + dot(a[1], b[0], dims))


def magnitude(index):
    return jnp.minimum(index, EXTENT - index)


def pick(position, entries):
    result = jnp.full_like(position, entries[0])
    for number, entry in enumerate(entries[1:], 1):
        result = jnp.where(position == number, entry, result)
    return result


def quarter_phase(value):
    row = lax.broadcasted_iota(jnp.int32, value.shape, 0)
    return jnp.where(row // 2 % 2 == 0, -pltpu.roll(value, 6, 0), pltpu.roll(value, 2, 0))


def body(
    orient, wedge, half, particle, shell, first_t, second_t, back_t, maps_ref, fsc_ref,
    source, first, second, back, slab_out, slab_in, tag_out, tag_in,
    sum_out, sum_in, count_out, count_in, row_out, row_in,
    load_sem, slab_s, slab_r, tag_s, tag_r, sum_s, sum_r, count_s, count_r, row_s, row_r,
):
    px, py = lax.axis_index("px"), lax.axis_index("py")
    me = px * SIDE + py
    loads = [
        pltpu.make_async_copy(a, b, load_sem.at[i])
        for i, (a, b) in enumerate(
            [(particle, source), (first_t, first), (second_t, second), (back_t, back)]
        )
    ]
    for load in loads:
        load.start()
    barrier = pltpu.get_barrier_semaphore()
    for k in range(1, SIDE):
        pl.semaphore_signal(
            barrier, 1, device_id=(px, lax.rem(py + k, SIDE)), device_id_type=MESH
        )
        pl.semaphore_signal(
            barrier, 1, device_id=(lax.rem(px + k, SIDE), py), device_id_type=MESH
        )

    turn, wedge_id, half_id = orient[0], wedge[0], half[0]
    quarter = turn % 4
    sign_x = (1 - 2 * ((quarter + 1) // 2 % 2)).astype(f32)
    sign_y = ((1 - 2 * (quarter // 2)) * (1 - 2 * (turn // 4))).astype(f32)
    swapped = turn % 2

    tag_row = lax.broadcasted_iota(jnp.int32, (4, 128), 0)
    tag_lane = lax.broadcasted_iota(jnp.int32, (4, 128), 1)
    limit = pick(jnp.broadcast_to(wedge_id, (4, 128)), THRESHOLDS) * swapped
    own_class = half_id * 8 + swapped * 4 + wedge_id
    tag = jnp.where(tag_row == 0, limit.astype(f32), 0.0)
    tag = jnp.where(tag_row == 1, jnp.broadcast_to(half_id, (4, 128)).astype(f32), tag)
    tag = jnp.where(tag_row == 2, jnp.broadcast_to(sign_y, (4, 128)), tag)
    tag = jnp.where(tag_row == 3, jnp.where(tag_lane == own_class, 1.0, 0.0), tag)
    tag_out[...] = tag
    tag_in[py] = tag

    row = lax.broadcasted_iota(jnp.int32, (EXTENT, EXTENT), 0)
    kx_abs = magnitude(row % SIDE * SIDE + row // SIDE)
    row_limit = pick(jnp.broadcast_to(wedge_id, (EXTENT, EXTENT)), THRESHOLDS) * (1 - swapped)
    row_mask = jnp.where(kx_abs >= row_limit, 1.0, 0.0)
    turned = jnp.broadcast_to(swapped, (BOX, BOX)) == 1
    loads[0].wait()
    loads[1].wait()
    for z in range(2):
        real, imag = source[0, z], source[1, z]
        real = jnp.where(turned, real.T, real)
        imag = jnp.where(turned, imag.T, imag)
        stacked = jnp.concatenate(
            [
                jnp.concatenate([real, imag * sign_y], 1),
                jnp.concatenate([imag * sign_x, real * (-sign_x * sign_y)], 1),
            ],
            0,
        )
        along = dot3((first[0], first[1]), cut(stacked), NN)
        if z == 0:
            along = along * row_mask
        slab_out[:, z * SIDE : (z + 1) * SIDE, :] = along.reshape(SIDE, SIDE, EXTENT)
    slab_in[py] = slab_out[py]
    pl.semaphore_wait(barrier, 2 * (SIDE - 1))

    sent = []
    for k in range(1, SIDE):
        other = lax.rem(py + k, SIDE)
        sent.append(
            pltpu.make_async_remote_copy(
                tag_out, tag_in.at[py], tag_s.at[k], tag_r.at[k], (px, other), MESH
            )
        )
        sent.append(
            pltpu.make_async_remote_copy(
                slab_out.at[other], slab_in.at[py], slab_s.at[k], slab_r.at[k], (px, other), MESH
            )
        )
    for copy in sent:
        copy.start()
    loads[2].wait()
    for copy in sent:
        copy.wait_recv()

    ky = lax.broadcasted_iota(jnp.int32, (1, EXTENT), 1)
    ky_abs = magnitude(ky).astype(f32)
    second_pair = (second[0], second[1])
    totals = [[jnp.zeros((SIDE, 2 * EXTENT), f32) for z in range(2)] for h in range(2)]
    counts = jnp.zeros((1, 128), f32)
    group = 4
    for start in range(0, SIDE, group):
        block = slab_in[start : start + group].reshape(group * 2 * SIDE, EXTENT)
        spread = dot3(cut(block), second_pair, NN)
        for g in range(group):
            tag = tag_in[start + g]
            lane_limit = jnp.concatenate([tag[0:1], tag[0:1]], 1)
            lane_half = jnp.concatenate([tag[1:2]] * 4, 1)
            lane_sign = jnp.concatenate([tag[2:3], tag[2:3]], 1)
            keep = jnp.where(ky_abs >= lane_limit, 1.0, 0.0)
            factors = (
                jnp.concatenate([keep, keep * lane_sign], 1),
                jnp.concatenate([jnp.ones_like(keep), lane_sign], 1),
            )
            counts = counts + tag[3:4]
            for z in range(2):
                base = (g * 2 + z) * SIDE
                value = spread[base : base + SIDE] * factors[z]
                upper = value * lane_half
                totals[1][z] = totals[1][z] + upper
                totals[0][z] = totals[0][z] + (value - upper)
    for h in range(2):
        for c in range(2):
            for z in range(2):
                sum_out[:, h * 4 + c * 2 + z, :] = totals[h][z][:, c * EXTENT : (c + 1) * EXTENT]
    count_out[...] = counts
    count_in[px] = counts
    sum_in[px] = sum_out[px]

    summed = []
    for k in range(1, SIDE):
        other = lax.rem(px + k, SIDE)
        summed.append(
            pltpu.make_async_remote_copy(
                count_out, count_in.at[px], count_s.at[k], count_r.at[k], (other, py), MESH
            )
        )
        summed.append(
            pltpu.make_async_remote_copy(
                sum_out.at[other], sum_in.at[px], sum_s.at[k], sum_r.at[k], (other, py), MESH
            )
        )
    for copy in summed:
        copy.start()
    loads[3].wait()

    comp = lax.broadcasted_iota(jnp.int32, (8, 128), 0)
    lane = lax.broadcasted_iota(jnp.int32, (8, 128), 1)
    kind = lax.broadcasted_iota(jnp.int32, (128, EXTENT), 0)
    ky_wide = magnitude(lax.broadcasted_iota(jnp.int32, (128, EXTENT), 1))
    reach = jnp.where(kind // 4 % 2 == 1, ky_wide, magnitude(me))
    inside = jnp.where(reach >= pick(kind % 4, THRESHOLDS), 1.0, 0.0).astype(bf16)
    number = lax.broadcasted_iota(jnp.int32, (128, EXTENT), 0) % NSHELL
    members = [jnp.where(number == shell[z], 1.0, 0.0).astype(bf16) for z in range(2)]
    for copy in summed:
        copy.wait_recv()
    total = sum_in[0]
    count = count_in[0]
    for k in range(1, SIDE):
        total = total + sum_in[k]
        count = count + count_in[k]
    by_half = jnp.where(lane // 8 == comp // 4, count, 0.0)
    masked_count = dot(by_half.astype(bf16), inside, NN)
    full_count = jnp.sum(by_half, axis=1, keepdims=True)
    wide_comp = lax.broadcasted_iota(jnp.int32, (8, EXTENT), 0)
    cover = jnp.where(wide_comp % 2 == 0, masked_count, full_count)
    average = total / jnp.maximum(cover, 1.0)

    powers = jnp.concatenate([average * average, average * pltpu.roll(average, 4, 0)], 0)
    powers = cut(powers)
    p_row = lax.broadcasted_iota(jnp.int32, (16, 128), 0)
    p_lane = lax.broadcasted_iota(jnp.int32, (16, 128), 1)
    wanted = jnp.where(p_row < 8, 1 + p_row // 4, jnp.where(p_row < 12, 0, 4))
    shells = jnp.zeros((1, 128), f32)
    for z in range(2):
        part = dot(powers[0], members[z], NT) + dot(powers[1], members[z], NT)
        part = jnp.where((p_row % 2 == z) & (p_lane // NSHELL == wanted), part, 0.0)
        shells = shells + jnp.sum(part, axis=0, keepdims=True)

    back_pair = (back[0], back[1])
    pair = jnp.concatenate([average, quarter_phase(average)], 1)
    padded = jnp.concatenate(
        [
            jnp.zeros((MAPLANE, 2 * EXTENT), f32),
            pair,
            jnp.zeros((128 - MAPLANE - 8, 2 * EXTENT), f32),
        ],
        0,
    )
    middle = dot3(back_pair, cut(padded), NT)
    row_out[...] = (middle + shells).reshape(EXTENT, 1, 128)
    row_in[me] = row_out[me]

    @pl.loop(1, EXTENT)
    def _(k):
        other = lax.rem(me + k, EXTENT)
        pltpu.make_async_remote_copy(
            row_out.at[other], row_in.at[me], row_s, row_r, (other // SIDE, other % SIDE), MESH
        ).start()

    whole = row_in.at[pl.ds(0, EXTENT - 1)]
    pltpu.make_async_copy(whole, whole, row_r).wait()
    rows = row_in[...].reshape(EXTENT, 128)
    sums = jnp.sum(rows, axis=0, keepdims=True)
    values = rows.T[MAPLANE : MAPLANE + 8]
    pair = jnp.concatenate([values, quarter_phase(values)], 1)
    final = dot3(cut(pair), back_pair, NT)
    for h in range(2):
        for c in range(2):
            for z in range(2):
                n = h * 4 + c * 2 + z
                maps_ref[h, c, z] = final[n : n + 1]
    sums = jnp.broadcast_to(sums, (8, 128))
    first_power = pltpu.roll(sums, 128 - NSHELL, 1)
    second_power = pltpu.roll(sums, 128 - 2 * NSHELL, 1)
    fsc_ref[...] = sums / (jnp.sqrt(first_power * second_power) + 1e-06)

    for copy in sent + summed:
        copy.wait_send()
    pltpu.make_async_copy(whole, whole, row_s).wait()


def shards(particles, orientation, wedge_index, half_set, shell_map):
    first, second, back = (halves(t) for t in tables())
    smem = pl.BlockSpec(memory_space=pltpu.SMEM)
    vmem = pl.BlockSpec(memory_space=pltpu.VMEM)
    hbm = pl.BlockSpec(memory_space=pl.ANY)
    dma = pltpu.SemaphoreType.DMA
    maps, fsc = pl.pallas_call(
        body,
        out_shape=(
            jax.ShapeDtypeStruct((2, 2, 2, 1, EXTENT), f32),
            jax.ShapeDtypeStruct((8, 128), f32),
        ),
        in_specs=[smem, smem, smem, hbm, vmem, hbm, hbm, hbm],
        out_specs=(vmem, vmem),
        scratch_shapes=[
            pltpu.VMEM((2, 2, BOX, BOX), f32),
            pltpu.VMEM((2, EXTENT, EXTENT), bf16),
            pltpu.VMEM((2, EXTENT, 2 * EXTENT), bf16),
            pltpu.VMEM((2, EXTENT, 2 * EXTENT), bf16),
            pltpu.VMEM((SIDE, 2 * SIDE, EXTENT), f32),
            pltpu.VMEM((SIDE, 2 * SIDE, EXTENT), f32),
            pltpu.VMEM((4, 128), f32),
            pltpu.VMEM((SIDE, 4, 128), f32),
            pltpu.VMEM((SIDE, 8, EXTENT), f32),
            pltpu.VMEM((SIDE, 8, EXTENT), f32),
            pltpu.VMEM((1, 128), f32),
            pltpu.VMEM((SIDE, 1, 128), f32),
            pltpu.VMEM((EXTENT, 1, 128), f32),
            pltpu.VMEM((EXTENT, 1, 128), f32),
            dma((4,)),
            dma((SIDE,)), dma((SIDE,)), dma((SIDE,)), dma((SIDE,)),
            dma((SIDE,)), dma((SIDE,)), dma((SIDE,)), dma((SIDE,)),
            dma, dma,
        ],
        compiler_params=pltpu.CompilerParams(collective_id=0, has_side_effects=True),
        name="subtomogram_average",
    )(orientation, wedge_index, half_set, particles[0], shell_map, first, second, back)
    return maps, fsc[0, :NSHELL]


def solution(mesh):
    both = ("px", "py")
    return jax.shard_map(
        shards,
        mesh=mesh,
        in_specs=(P(both, None, None, None, None), P(both), P(both), P(both), P(None, both, None)),
        out_specs=(P(None, None, None, both, None), P()),
        check_vma=False,
    )
```

time: 363 us -> 46.4 us (0.13)
  waiting for transfers between devices: 252 us -> 0 us
  blocking collectives: 45.8 us -> 0 us
  Pallas kernels: 0 us -> 41.1 us
  local copies, waits for them, and re-layouts: 16.8 us -> 2.48 us
  between operations: 16.1 us -> 2.57 us
  other arithmetic: 11.7 us -> 0 us
  matrix products: 10.4 us -> 0 us
  starting transfers between devices: 9.85 us -> 0 us
    unnamed x4 -> x0, waiting for transfers between devices: 224 us -> none
    psum x5 -> x0, blocking collectives: 45.8 us -> none  [over_axes(): value = lax.psum(value, axis)]
    pallas_call x0 -> x1, Pallas kernels: none -> 41.1 us  [shards(): pl.pallas_call(body, out_shape=(jax.ShapeDtypeStruct((2, 2, 2, 1, EXTENT)...]
    reduce_scatter x2 -> x0, waiting for transfers between devices: 22.6 us -> none  [scatter_pairs(): tiles = lax.psum_scatter(tiles, core, scatter_dimension=0, tiled=True)]
    dot_general x9 -> x0, matrix products: 10.4 us -> none  [the longest x1 1.46 us: shards(): jnp.einsum('czak,aj->czjk', partial_turn, cos_fwd, precision=highest)]
    all_to_all x2 -> x0, starting transfers between devices: 9.55 us -> none  [the longest x1 5.94 us: shards(): lax.all_to_all(middle, PX, split_axis=3, concat_axis=4, tiled=True)]
    reduce_scatter x2 -> x0, local copies, waits for them, and re-layouts: 5.26 us -> none  [scatter_pairs(): tiles = lax.psum_scatter(tiles, core, scatter_dimension=0, tiled=True)]
    all_to_all x2 -> x0, waiting for transfers between devices: 4.97 us -> none  [the longest x1 4.96 us: shards(): lax.all_to_all(lax.all_to_all(middle, PX, split_axis=3, concat_axis=4, ti...]
  transfers between devices with their start and end apart: 5 -> 0, of which waited for: 4 -> 0; matrix products, arithmetic and copies ran while one was open for 4% -> 0% of each run, Pallas kernels for 0% -> 0%
where the time goes in v1:
time: 46.4 us; the launch traced here: 46.2 us
  Pallas kernels  41.1 us (89%)
  between operations  2.57 us (6%)
  local copies, waits for them, and re-layouts  2.48 us (5%)
    pallas_call x1, Pallas kernels, shards(): pl.pallas_call(body, out_shape=(jax.ShapeDtypeStruct((2, 2, 2, 1, EXTENT)...  41.1 us
    unnamed x1, local copies, waits for them, and re-layouts  1.29 us
    squeeze x1, local copies, waits for them, and re-layouts, shards(): return (maps, fsc[0, :NSHELL])  1.18 us

profile of v1, /device:TPU:1, one launch (start us, length us, event | category | flops | bytes accessed | tf_op | source)
XLA Modules:
  0.0 46.2 jit_solution(12496354911398008510)
XLA Ops:
  2.6 41.1 %subtomogram_average.1 = (f32[2,2,2,1,256]{4,3,2,1,0:T(1,128)}, f32[8,128]{1,0:T(8,128)}) custom-call(s32[1]{0:T(128)S(6)} %copy.11.orient, s32[1]{0:T(128)S(6)} %copy.12.wedge, s32[1]{0:T(128)S(6)} %copy.13.half, f32[2,2,128,128]{3,2,1,0:T(8,128)} %bitcast.3, s32[2,1,256]{2,1,0:T(1,128)} %shell.1, bf16[2,256,256]{2,1,0:T(8,128)(2,1)} %constant.20.first_t, ...), custom_call_target="tpu_custom_call" | custom-call | tf_op jit(solution)/shard_map/subtomogram_average/pallas_call | solution.py:300
  43.7 1.2 %slice_bitcast_fusion = f32[32]{0:T(128)} fusion(f32[8,128]{1,0:T(8,128)} %get-tuple-element.5), kind=kLoop, calls=%fused_computation | loop fusion | bytes 256 | tf_op jit(solution)/shard_map/squeeze | solution.py:331
  44.9 1.3 %copy.14 = f32[2,2,2,1,256]{4,3,2,1,0:T(1,128)} copy(f32[2,2,2,1,256]{4,3,2,1,0:T(1,128)} %get-tuple-element.8) | data formatting | bytes 16384

commit v2 on v1

--- a/solution.py
+++ b/solution.py
@@ -12,7 +12,9 @@
 RISE = (1, 3, 2, 3)
 RUN = (1, 2, 1, 1)
 NSHELL = 32
-SIDE = 16
+PLANE = 32
+DEPTH = 8
+LINE = 16
 EXTENT = 256
 BOX = 128
 KZ = 128
@@ -37,8 +39,8 @@
     cell = np.arange(BOX) - BOX // 2
     scale = 1.0 / math.sqrt(EXTENT)
     unit = 2.0 * math.pi / EXTENT
-    rows = np.arange(SIDE)
-    order = (rows[None, :] * SIDE + rows[:, None]).reshape(-1)
+    place, level = np.arange(PLANE)[:, None], np.arange(DEPTH)[None, :]
+    order = (place // LINE * (LINE * DEPTH) + level * LINE + place % LINE).reshape(-1)
     angle = (order[:, None] * cell[None, :] % EXTENT) * unit
     first = np.concatenate([np.cos(angle), np.sin(angle)], 1) * scale
     angle = (cell[:, None] * freq[None, :] % EXTENT) * unit
@@ -83,9 +85,20 @@
     source, first, second, back, slab_out, slab_in, tag_out, tag_in,
     sum_out, sum_in, count_out, count_in, row_out, row_in,
     load_sem, slab_s, slab_r, tag_s, tag_r, sum_s, sum_r, count_s, count_r, row_s, row_r,
+    above_sem, below_sem,
 ):
     px, py = lax.axis_index("px"), lax.axis_index("py")
-    me = px * SIDE + py
+    me = px * LINE + py
+    side, level = lax.div(px, DEPTH), lax.rem(px, DEPTH)
+    place = side * LINE + py
+    sides = [side, 1 - side]
+    lines = [py] + [lax.rem(py + b, LINE) for b in range(1, LINE)]
+    far_first = [8, 9, 10, 11, 7, 6, 5, 4, 12, 13, 14, 15, 3, 2, 1, 0]
+    plane = [(sides[a], lines[b]) for b in far_first for a in (1, 0)][:-1]
+    levels = [level] + [lax.rem(level + c, DEPTH) for c in range(1, DEPTH)]
+    column = [levels[c] for c in (4, 3, 5, 2, 6, 1, 7)]
+    above = (side * DEPTH + levels[1], py)
+    below = (side * DEPTH + levels[7], py)
     loads = [
         pltpu.make_async_copy(a, b, load_sem.at[i])
         for i, (a, b) in enumerate(
@@ -95,13 +108,10 @@
     for load in loads:
         load.start()
     barrier = pltpu.get_barrier_semaphore()
-    for k in range(1, SIDE):
-        pl.semaphore_signal(
-            barrier, 1, device_id=(px, lax.rem(py + k, SIDE)), device_id_type=MESH
-        )
-        pl.semaphore_signal(
-            barrier, 1, device_id=(lax.rem(px + k, SIDE), py), device_id_type=MESH
-        )
+    for a, b in plane:
+        pl.semaphore_signal(barrier, 1, device_id=(a * DEPTH + level, b), device_id_type=MESH)
+    for neighbour in (above, below):
+        pl.semaphore_signal(barrier, 1, device_id=neighbour, device_id_type=MESH)
 
     turn, wedge_id, half_id = orient[0], wedge[0], half[0]
     quarter = turn % 4
@@ -118,10 +128,11 @@
     tag = jnp.where(tag_row == 2, jnp.broadcast_to(sign_y, (4, 128)), tag)
     tag = jnp.where(tag_row == 3, jnp.where(tag_lane == own_class, 1.0, 0.0), tag)
     tag_out[...] = tag
-    tag_in[py] = tag
+    tag_in[place] = tag
 
     row = lax.broadcasted_iota(jnp.int32, (EXTENT, EXTENT), 0)
-    kx_abs = magnitude(row % SIDE * SIDE + row // SIDE)
+    kx = row // (DEPTH * LINE) * (DEPTH * LINE) + row % DEPTH * LINE + row // DEPTH % LINE
+    kx_abs = magnitude(kx)
     row_limit = pick(jnp.broadcast_to(wedge_id, (EXTENT, EXTENT)), THRESHOLDS) * (1 - swapped)
     row_mask = jnp.where(kx_abs >= row_limit, 1.0, 0.0)
     turned = jnp.broadcast_to(swapped, (BOX, BOX)) == 1
@@ -141,25 +152,31 @@
         along = dot3((first[0], first[1]), cut(stacked), NN)
         if z == 0:
             along = along * row_mask
-        slab_out[:, z * SIDE : (z + 1) * SIDE, :] = along.reshape(SIDE, SIDE, EXTENT)
-    slab_in[py] = slab_out[py]
-    pl.semaphore_wait(barrier, 2 * (SIDE - 1))
+        slab_out[:, z * DEPTH : (z + 1) * DEPTH, :] = along.reshape(PLANE, DEPTH, EXTENT)
+    slab_in[place] = slab_out[place]
+    pl.semaphore_wait(barrier, PLANE + 1)
 
     sent = []
-    for k in range(1, SIDE):
-        other = lax.rem(py + k, SIDE)
+    for k, (a, b) in enumerate(plane):
+        to = (a * DEPTH + level, b)
         sent.append(
             pltpu.make_async_remote_copy(
-                tag_out, tag_in.at[py], tag_s.at[k], tag_r.at[k], (px, other), MESH
+                tag_out, tag_in.at[place], tag_s.at[k], tag_r.at[k], to, MESH
             )
         )
         sent.append(
             pltpu.make_async_remote_copy(
-                slab_out.at[other], slab_in.at[py], slab_s.at[k], slab_r.at[k], (px, other), MESH
+                slab_out.at[a * LINE + b], slab_in.at[place], slab_s.at[k], slab_r.at[k], to, MESH
             )
         )
     for copy in sent:
         copy.start()
+    for step in range(3):
+        pl.semaphore_signal(above_sem.at[step], 1, device_id=above, device_id_type=MESH)
+        if step < 2:
+            pl.semaphore_signal(below_sem.at[step], 1, device_id=below, device_id_type=MESH)
+            pl.semaphore_wait(below_sem.at[step], 1)
+        pl.semaphore_wait(above_sem.at[step], 1)
     loads[2].wait()
     for copy in sent:
         copy.wait_recv()
@@ -167,11 +184,11 @@
     ky = lax.broadcasted_iota(jnp.int32, (1, EXTENT), 1)
     ky_abs = magnitude(ky).astype(f32)
     second_pair = (second[0], second[1])
-    totals = [[jnp.zeros((SIDE, 2 * EXTENT), f32) for z in range(2)] for h in range(2)]
+    totals = [[jnp.zeros((DEPTH, 2 * EXTENT), f32) for z in range(2)] for h in range(2)]
     counts = jnp.zeros((1, 128), f32)
-    group = 4
-    for start in range(0, SIDE, group):
-        block = slab_in[start : start + group].reshape(group * 2 * SIDE, EXTENT)
+    group = 8
+    for start in range(0, PLANE, group):
+        block = slab_in[start : start + group].reshape(group * 2 * DEPTH, EXTENT)
         spread = dot3(cut(block), second_pair, NN)
         for g in range(group):
             tag = tag_in[start + g]
@@ -185,8 +202,8 @@
             )
             counts = counts + tag[3:4]
             for z in range(2):
-                base = (g * 2 + z) * SIDE
-                value = spread[base : base + SIDE] * factors[z]
+                base = (g * 2 + z) * DEPTH
+                value = spread[base : base + DEPTH] * factors[z]
                 upper = value * lane_half
                 totals[1][z] = totals[1][z] + upper
                 totals[0][z] = totals[0][z] + (value - upper)
@@ -195,20 +212,20 @@
             for z in range(2):
                 sum_out[:, h * 4 + c * 2 + z, :] = totals[h][z][:, c * EXTENT : (c + 1) * EXTENT]
     count_out[...] = counts
-    count_in[px] = counts
-    sum_in[px] = sum_out[px]
+    count_in[level] = counts
+    sum_in[level] = sum_out[level]
 
     summed = []
-    for k in range(1, SIDE):
-        other = lax.rem(px + k, SIDE)
+    for k, other in enumerate(column):
+        to = (side * DEPTH + other, py)
         summed.append(
             pltpu.make_async_remote_copy(
-                count_out, count_in.at[px], count_s.at[k], count_r.at[k], (other, py), MESH
+                count_out, count_in.at[level], count_s.at[k], count_r.at[k], to, MESH
             )
         )
         summed.append(
             pltpu.make_async_remote_copy(
-                sum_out.at[other], sum_in.at[px], sum_s.at[k], sum_r.at[k], (other, py), MESH
+                sum_out.at[other], sum_in.at[level], sum_s.at[k], sum_r.at[k], to, MESH
             )
         )
     for copy in summed:
@@ -227,7 +244,7 @@
         copy.wait_recv()
     total = sum_in[0]
     count = count_in[0]
-    for k in range(1, SIDE):
+    for k in range(1, DEPTH):
         total = total + sum_in[k]
         count = count + count_in[k]
     by_half = jnp.where(lane // 8 == comp // 4, count, 0.0)
@@ -259,19 +276,30 @@
         0,
     )
     middle = dot3(back_pair, cut(padded), NT)
-    row_out[...] = (middle + shells).reshape(EXTENT, 1, 128)
-    row_in[me] = row_out[me]
-
-    @pl.loop(1, EXTENT)
-    def _(k):
-        other = lax.rem(me + k, EXTENT)
+    row_out[...] = middle + shells
+    row_in[pl.ds(me, 1)] = row_out[pl.ds(me, 1)]
+
+    def send_row(a, c, b):
+        to = (a * DEPTH + c, b)
+        other = to[0] * LINE + b
         pltpu.make_async_remote_copy(
-            row_out.at[other], row_in.at[me], row_s, row_r, (other // SIDE, other % SIDE), MESH
+            row_out.at[pl.ds(other, 1)], row_in.at[pl.ds(me, 1)], row_s, row_r, to, MESH
         ).start()
+
+    @pl.loop(0, DEPTH - 1)
+    def _(step):
+        away = lax.div(step + 1, 2)
+        shift = away * (1 - 2 * lax.rem(step, 2))
+        other = lax.rem(level + 12 + shift, DEPTH)
+        for a, b in plane + [(side, py)]:
+            send_row(a, other, b)
+
+    for a, b in plane:
+        send_row(a, level, b)
 
     whole = row_in.at[pl.ds(0, EXTENT - 1)]
     pltpu.make_async_copy(whole, whole, row_r).wait()
-    rows = row_in[...].reshape(EXTENT, 128)
+    rows = row_in[...]
     sums = jnp.sum(rows, axis=0, keepdims=True)
     values = rows.T[MAPLANE : MAPLANE + 8]
     pair = jnp.concatenate([values, quarter_phase(values)], 1)
@@ -310,20 +338,21 @@
             pltpu.VMEM((2, EXTENT, EXTENT), bf16),
             pltpu.VMEM((2, EXTENT, 2 * EXTENT), bf16),
             pltpu.VMEM((2, EXTENT, 2 * EXTENT), bf16),
-            pltpu.VMEM((SIDE, 2 * SIDE, EXTENT), f32),
-            pltpu.VMEM((SIDE, 2 * SIDE, EXTENT), f32),
+            pltpu.VMEM((PLANE, 2 * DEPTH, EXTENT), f32),
+            pltpu.VMEM((PLANE, 2 * DEPTH, EXTENT), f32),
             pltpu.VMEM((4, 128), f32),
-            pltpu.VMEM((SIDE, 4, 128), f32),
-            pltpu.VMEM((SIDE, 8, EXTENT), f32),
-            pltpu.VMEM((SIDE, 8, EXTENT), f32),
+            pltpu.VMEM((PLANE, 4, 128), f32),
+            pltpu.VMEM((DEPTH, 8, EXTENT), f32),
+            pltpu.VMEM((DEPTH, 8, EXTENT), f32),
             pltpu.VMEM((1, 128), f32),
-            pltpu.VMEM((SIDE, 1, 128), f32),
-            pltpu.VMEM((EXTENT, 1, 128), f32),
-            pltpu.VMEM((EXTENT, 1, 128), f32),
+            pltpu.VMEM((DEPTH, 1, 128), f32),
+            pltpu.VMEM((EXTENT, 128), f32),
+            pltpu.VMEM((EXTENT, 128), f32),
             dma((4,)),
-            dma((SIDE,)), dma((SIDE,)), dma((SIDE,)), dma((SIDE,)),
-            dma((SIDE,)), dma((SIDE,)), dma((SIDE,)), dma((SIDE,)),
+            dma((PLANE,)), dma((PLANE,)), dma((PLANE,)), dma((PLANE,)),
+            dma((DEPTH,)), dma((DEPTH,)), dma((DEPTH,)), dma((DEPTH,)),
             dma, dma,
+            pltpu.SemaphoreType.REGULAR((3,)), pltpu.SemaphoreType.REGULAR((2,)),
         ],
         compiler_params=pltpu.CompilerParams(collective_id=0, has_side_effects=True),
         name="subtomogram_average",

time: 46.4 us -> 40.8 us (0.88)
  Pallas kernels: 41.1 us -> 35.5 us
    pallas_call x1, Pallas kernels: 41.1 us -> 35.5 us  [shards(): pl.pallas_call(body, out_shape=(jax.ShapeDtypeStruct((2, 2, 2, 1, EXTENT)...]
where the time goes in v2:
time: 40.8 us; the launch traced here: 40.6 us
  Pallas kernels  35.5 us (87%)
  between operations  2.57 us (6%)
  local copies, waits for them, and re-layouts  2.48 us (6%)
    pallas_call x1, Pallas kernels, shards(): pl.pallas_call(body, out_shape=(jax.ShapeDtypeStruct((2, 2, 2, 1, EXTENT)...  35.5 us
    unnamed x1, local copies, waits for them, and re-layouts  1.29 us
    squeeze x1, local copies, waits for them, and re-layouts, shards(): return (maps, fsc[0, :NSHELL])  1.18 us

profile of v2, /device:TPU:1, one launch (start us, length us, event | category | flops | bytes accessed | tf_op | source)
XLA Modules:
  0.0 40.6 jit_solution(17884271389390302033)
XLA Ops:
  2.6 35.5 %subtomogram_average.1 = (f32[2,2,2,1,256]{4,3,2,1,0:T(1,128)}, f32[8,128]{1,0:T(8,128)}) custom-call(s32[1]{0:T(128)S(6)} %copy.11.orient, s32[1]{0:T(128)S(6)} %copy.12.wedge, s32[1]{0:T(128)S(6)} %copy.13.half, f32[2,2,128,128]{3,2,1,0:T(8,128)} %bitcast.3, s32[2,1,256]{2,1,0:T(1,128)} %shell.1, bf16[2,256,256]{2,1,0:T(8,128)(2,1)} %constant.20.first_t, ...), custom_call_target="tpu_custom_call" | custom-call | tf_op jit(solution)/shard_map/subtomogram_average/pallas_call | solution.py:328
  38.1 1.2 %slice_bitcast_fusion = f32[32]{0:T(128)} fusion(f32[8,128]{1,0:T(8,128)} %get-tuple-element.5), kind=kLoop, calls=%fused_computation | loop fusion | bytes 256 | tf_op jit(solution)/shard_map/squeeze | solution.py:360
  39.3 1.3 %copy.14 = f32[2,2,2,1,256]{4,3,2,1,0:T(1,128)} copy(f32[2,2,2,1,256]{4,3,2,1,0:T(1,128)} %get-tuple-element.8) | data formatting | bytes 16384

commit v3 on v2

--- a/solution.py
+++ b/solution.py
@@ -25,6 +25,9 @@
 NT = (((1,), (1,)), ((), ()))
 NN = (((1,), (0,)), ((), ()))
 MAPLANE = 96
+TAG = 2 * 2 * DEPTH
+SLAB = TAG + 1
+SIGN = 16
 
 
 def halves(table):
@@ -48,7 +51,14 @@
     second = np.block([[cosine, -sine], [sine, cosine]])
     angle = (freq[:, None] * freq[None, :] % EXTENT) * unit
     back = np.concatenate([np.cos(angle), np.sin(angle)], 1) * scale
-    return [np.asarray(t, np.float32) for t in (first, second, back)]
+    spread = np.zeros((128, 2 * EXTENT), np.float32)
+    size = np.minimum(freq, EXTENT - freq)
+    for kind in range(SIGN):
+        keep = size >= THRESHOLDS[kind % 4] if kind // 4 % 2 else size >= 0
+        spread[kind, :EXTENT] = keep
+        spread[kind, EXTENT : EXTENT + 128] = kind // 8
+    spread[SIGN, EXTENT + 128 :] = 1.0
+    return [np.asarray(t, np.float32) for t in (first, second, back, spread)]
 
 
 def cut(value):
@@ -81,10 +91,11 @@
 
 
 def body(
-    orient, wedge, half, particle, shell, first_t, second_t, back_t, maps_ref, fsc_ref,
-    source, first, second, back, slab_out, slab_in, tag_out, tag_in,
-    sum_out, sum_in, count_out, count_in, row_out, row_in,
-    load_sem, slab_s, slab_r, tag_s, tag_r, sum_s, sum_r, count_s, count_r, row_s, row_r,
+    orient_t, wedge_t, half_t, particle, shell_t, first_t, second_t, back_t, spread_t,
+    maps_ref, fsc_ref,
+    orient, wedge, half, source, shell, first, second, back, spread, slab_out, slab_in,
+    sum_out, sum_in, count_out, count_in, row_out, row_in, inside_ref, member_ref,
+    load_sem, slab_s, slab_r, sum_s, sum_r, count_s, count_r, row_s, row_r,
     above_sem, below_sem,
 ):
     px, py = lax.axis_index("px"), lax.axis_index("py")
@@ -94,18 +105,19 @@
     sides = [side, 1 - side]
     lines = [py] + [lax.rem(py + b, LINE) for b in range(1, LINE)]
     far_first = [8, 9, 10, 11, 7, 6, 5, 4, 12, 13, 14, 15, 3, 2, 1, 0]
-    plane = [(sides[a], lines[b]) for b in far_first for a in (1, 0)][:-1]
+    offsets = [(a, b) for b in far_first for a in (1, 0)][:-1]
+    plane = [(sides[a], lines[b]) for a, b in offsets]
+    slots = [offsets.index((a, (LINE - b) % LINE)) for a, b in offsets]
     levels = [level] + [lax.rem(level + c, DEPTH) for c in range(1, DEPTH)]
     column = [levels[c] for c in (4, 3, 5, 2, 6, 1, 7)]
     above = (side * DEPTH + levels[1], py)
     below = (side * DEPTH + levels[7], py)
-    loads = [
-        pltpu.make_async_copy(a, b, load_sem.at[i])
-        for i, (a, b) in enumerate(
-            [(particle, source), (first_t, first), (second_t, second), (back_t, back)]
-        )
+    pairs = [
+        (particle, source), (first_t, first), (orient_t, orient), (wedge_t, wedge),
+        (half_t, half), (second_t, second), (spread_t, spread), (shell_t, shell), (back_t, back),
     ]
-    for load in loads:
+    loads = [pltpu.make_async_copy(a, b, load_sem.at[i]) for i, (a, b) in enumerate(pairs)]
+    for load in loads[:5]:
         load.start()
     barrier = pltpu.get_barrier_semaphore()
     for a, b in plane:
@@ -113,27 +125,26 @@
     for neighbour in (above, below):
         pl.semaphore_signal(barrier, 1, device_id=neighbour, device_id_type=MESH)
 
+    for load in loads[5:]:
+        load.start()
+    for load in loads[2:5]:
+        load.wait()
     turn, wedge_id, half_id = orient[0], wedge[0], half[0]
     quarter = turn % 4
     sign_x = (1 - 2 * ((quarter + 1) // 2 % 2)).astype(f32)
     sign_y = ((1 - 2 * (quarter // 2)) * (1 - 2 * (turn // 4))).astype(f32)
     swapped = turn % 2
 
-    tag_row = lax.broadcasted_iota(jnp.int32, (4, 128), 0)
-    tag_lane = lax.broadcasted_iota(jnp.int32, (4, 128), 1)
-    limit = pick(jnp.broadcast_to(wedge_id, (4, 128)), THRESHOLDS) * swapped
+    lane = lax.broadcasted_iota(jnp.int32, (PLANE, 128), 1)
     own_class = half_id * 8 + swapped * 4 + wedge_id
-    tag = jnp.where(tag_row == 0, limit.astype(f32), 0.0)
-    tag = jnp.where(tag_row == 1, jnp.broadcast_to(half_id, (4, 128)).astype(f32), tag)
-    tag = jnp.where(tag_row == 2, jnp.broadcast_to(sign_y, (4, 128)), tag)
-    tag = jnp.where(tag_row == 3, jnp.where(tag_lane == own_class, 1.0, 0.0), tag)
-    tag_out[...] = tag
-    tag_in[place] = tag
-
-    row = lax.broadcasted_iota(jnp.int32, (EXTENT, EXTENT), 0)
+    tag = jnp.where(lane == own_class, 1.0, 0.0)
+    tag = jnp.where(lane == SIGN, jnp.broadcast_to(sign_y, (PLANE, 128)), tag)
+    slab_out[:, TAG, :] = tag
+
+    row = lax.broadcasted_iota(jnp.int32, (EXTENT, 128), 0)
     kx = row // (DEPTH * LINE) * (DEPTH * LINE) + row % DEPTH * LINE + row // DEPTH % LINE
     kx_abs = magnitude(kx)
-    row_limit = pick(jnp.broadcast_to(wedge_id, (EXTENT, EXTENT)), THRESHOLDS) * (1 - swapped)
+    row_limit = pick(jnp.broadcast_to(wedge_id, (EXTENT, 128)), THRESHOLDS) * (1 - swapped)
     row_mask = jnp.where(kx_abs >= row_limit, 1.0, 0.0)
     turned = jnp.broadcast_to(swapped, (BOX, BOX)) == 1
     loads[0].wait()
@@ -151,22 +162,21 @@
         )
         along = dot3((first[0], first[1]), cut(stacked), NN)
         if z == 0:
-            along = along * row_mask
-        slab_out[:, z * DEPTH : (z + 1) * DEPTH, :] = along.reshape(PLANE, DEPTH, EXTENT)
-    slab_in[place] = slab_out[place]
+            along = along * jnp.concatenate([row_mask, row_mask], 1)
+        for c in range(2):
+            base = (2 * z + c) * DEPTH
+            slab_out[:, base : base + DEPTH, :] = along[:, c * 128 : (c + 1) * 128].reshape(
+                PLANE, DEPTH, 128
+            )
+    slab_in[PLANE - 1] = slab_out[place]
     pl.semaphore_wait(barrier, PLANE + 1)
 
     sent = []
     for k, (a, b) in enumerate(plane):
-        to = (a * DEPTH + level, b)
         sent.append(
             pltpu.make_async_remote_copy(
-                tag_out, tag_in.at[place], tag_s.at[k], tag_r.at[k], to, MESH
-            )
-        )
-        sent.append(
-            pltpu.make_async_remote_copy(
-                slab_out.at[a * LINE + b], slab_in.at[place], slab_s.at[k], slab_r.at[k], to, MESH
+                slab_out.at[a * LINE + b, pl.ds(0, SLAB)], slab_in.at[slots[k], pl.ds(0, SLAB)],
+                slab_s.at[k], slab_r.at[slots[k]], (a * DEPTH + level, b), MESH,
             )
         )
     for copy in sent:
@@ -177,33 +187,46 @@
             pl.semaphore_signal(below_sem.at[step], 1, device_id=below, device_id_type=MESH)
             pl.semaphore_wait(below_sem.at[step], 1)
         pl.semaphore_wait(above_sem.at[step], 1)
-    loads[2].wait()
-    for copy in sent:
-        copy.wait_recv()
-
-    ky = lax.broadcasted_iota(jnp.int32, (1, EXTENT), 1)
-    ky_abs = magnitude(ky).astype(f32)
+    kind = lax.broadcasted_iota(jnp.int32, (128, EXTENT), 0)
+    ky_wide = magnitude(lax.broadcasted_iota(jnp.int32, (128, EXTENT), 1))
+    reach = jnp.where(kind // 4 % 2 == 1, ky_wide, magnitude(me))
+    inside_ref[...] = jnp.where(reach >= pick(kind % 4, THRESHOLDS), 1.0, 0.0).astype(bf16)
+    for load in loads[5:]:
+        load.wait()
+    number = kind % NSHELL
+    for z in range(2):
+        member_ref[z] = jnp.where(number == shell[z], 1.0, 0.0).astype(bf16)
+
     second_pair = (second[0], second[1])
+    spread_map = spread[...]
     totals = [[jnp.zeros((DEPTH, 2 * EXTENT), f32) for z in range(2)] for h in range(2)]
     counts = jnp.zeros((1, 128), f32)
     group = 8
-    for start in range(0, PLANE, group):
-        block = slab_in[start : start + group].reshape(group * 2 * DEPTH, EXTENT)
-        spread = dot3(cut(block), second_pair, NN)
+    arrivals = {slots[k]: copy for k, copy in enumerate(sent)}
+    for start in range(PLANE - group, -1, -group):
+        for k in range(start, min(start + group, PLANE - 1)):
+            arrivals[k].wait_recv()
+        tags = slab_in[start : start + group, TAG, :]
+        counts = counts + jnp.sum(tags, axis=0, keepdims=True)
+        vectors = dot(tags.astype(bf16), spread_map, NN)
+        blocks = []
+        for z in range(2):
+            real = slab_in[start : start + group, 2 * z * DEPTH : (2 * z + 1) * DEPTH, :]
+            imag = slab_in[start : start + group, (2 * z + 1) * DEPTH : (2 * z + 2) * DEPTH, :]
+            blocks.append(jnp.concatenate([real, imag], 2).reshape(group * DEPTH, EXTENT))
+        waves = dot3(cut(jnp.concatenate(blocks, 0)), second_pair, NN)
         for g in range(group):
-            tag = tag_in[start + g]
-            lane_limit = jnp.concatenate([tag[0:1], tag[0:1]], 1)
-            lane_half = jnp.concatenate([tag[1:2]] * 4, 1)
-            lane_sign = jnp.concatenate([tag[2:3], tag[2:3]], 1)
-            keep = jnp.where(ky_abs >= lane_limit, 1.0, 0.0)
+            vector = vectors[g : g + 1]
+            keep = vector[:, :EXTENT]
+            lane_half = jnp.concatenate([vector[:, EXTENT : EXTENT + 128]] * 4, 1)
+            lane_sign = jnp.concatenate([vector[:, EXTENT + 128 :]] * 2, 1)
             factors = (
                 jnp.concatenate([keep, keep * lane_sign], 1),
                 jnp.concatenate([jnp.ones_like(keep), lane_sign], 1),
             )
-            counts = counts + tag[3:4]
             for z in range(2):
-                base = (g * 2 + z) * DEPTH
-                value = spread[base : base + DEPTH] * factors[z]
+                base = (z * group + g) * DEPTH
+                value = waves[base : base + DEPTH] * factors[z]
                 upper = value * lane_half
                 totals[1][z] = totals[1][z] + upper
                 totals[0][z] = totals[0][z] + (value - upper)
@@ -230,16 +253,10 @@
         )
     for copy in summed:
         copy.start()
-    loads[3].wait()
-
     comp = lax.broadcasted_iota(jnp.int32, (8, 128), 0)
     lane = lax.broadcasted_iota(jnp.int32, (8, 128), 1)
-    kind = lax.broadcasted_iota(jnp.int32, (128, EXTENT), 0)
-    ky_wide = magnitude(lax.broadcasted_iota(jnp.int32, (128, EXTENT), 1))
-    reach = jnp.where(kind // 4 % 2 == 1, ky_wide, magnitude(me))
-    inside = jnp.where(reach >= pick(kind % 4, THRESHOLDS), 1.0, 0.0).astype(bf16)
-    number = lax.broadcasted_iota(jnp.int32, (128, EXTENT), 0) % NSHELL
-    members = [jnp.where(number == shell[z], 1.0, 0.0).astype(bf16) for z in range(2)]
+    inside = inside_ref[...]
+    members = [member_ref[0], member_ref[1]]
     for copy in summed:
         copy.wait_recv()
     total = sum_in[0]
@@ -304,60 +321,82 @@
     values = rows.T[MAPLANE : MAPLANE + 8]
     pair = jnp.concatenate([values, quarter_phase(values)], 1)
     final = dot3(cut(pair), back_pair, NT)
+    maps_ref[...] = final
+    sums = jnp.broadcast_to(sums, (8, 128))
+    first_power = pltpu.roll(sums, 128 - NSHELL, 1)
+    second_power = pltpu.roll(sums, 128 - 2 * NSHELL, 1)
+    fsc_ref[...] = sums / (jnp.sqrt(first_power * second_power) + 1e-06)
+
+    for copy in sent + summed:
+        copy.wait_send()
+    pltpu.make_async_copy(whole, whole, row_s).wait()
+
+
+def finish(final, shells, maps_ref, fsc_ref):
     for h in range(2):
         for c in range(2):
             for z in range(2):
                 n = h * 4 + c * 2 + z
                 maps_ref[h, c, z] = final[n : n + 1]
-    sums = jnp.broadcast_to(sums, (8, 128))
-    first_power = pltpu.roll(sums, 128 - NSHELL, 1)
-    second_power = pltpu.roll(sums, 128 - 2 * NSHELL, 1)
-    fsc_ref[...] = sums / (jnp.sqrt(first_power * second_power) + 1e-06)
-
-    for copy in sent + summed:
-        copy.wait_send()
-    pltpu.make_async_copy(whole, whole, row_s).wait()
+    fsc_ref[...] = shells[0, :NSHELL]
 
 
 def shards(particles, orientation, wedge_index, half_set, shell_map):
-    first, second, back = (halves(t) for t in tables())
-    smem = pl.BlockSpec(memory_space=pltpu.SMEM)
+    first, second, back, spread = tables()
+    first, second, back = (halves(t) for t in (first, second, back))
+    spread = jnp.asarray(spread, bf16)
     vmem = pl.BlockSpec(memory_space=pltpu.VMEM)
-    hbm = pl.BlockSpec(memory_space=pl.ANY)
+    hbm = pl.BlockSpec(memory_space=pltpu.HBM)
     dma = pltpu.SemaphoreType.DMA
-    maps, fsc = pl.pallas_call(
+    final, shells = pl.pallas_call(
         body,
         out_shape=(
-            jax.ShapeDtypeStruct((2, 2, 2, 1, EXTENT), f32),
-            jax.ShapeDtypeStruct((8, 128), f32),
+            pltpu.VMEM((8, EXTENT), f32),
+            pltpu.VMEM((8, 128), f32),
         ),
-        in_specs=[smem, smem, smem, hbm, vmem, hbm, hbm, hbm],
+        in_specs=[hbm] * 9,
         out_specs=(vmem, vmem),
         scratch_shapes=[
+            pltpu.SMEM((1,), jnp.int32), pltpu.SMEM((1,), jnp.int32), pltpu.SMEM((1,), jnp.int32),
             pltpu.VMEM((2, 2, BOX, BOX), f32),
+            pltpu.VMEM((2, 1, EXTENT), jnp.int32),
             pltpu.VMEM((2, EXTENT, EXTENT), bf16),
             pltpu.VMEM((2, EXTENT, 2 * EXTENT), bf16),
             pltpu.VMEM((2, EXTENT, 2 * EXTENT), bf16),
-            pltpu.VMEM((PLANE, 2 * DEPTH, EXTENT), f32),
-            pltpu.VMEM((PLANE, 2 * DEPTH, EXTENT), f32),
-            pltpu.VMEM((4, 128), f32),
-            pltpu.VMEM((PLANE, 4, 128), f32),
+            pltpu.VMEM((128, 2 * EXTENT), bf16),
+            pltpu.VMEM((PLANE, SLAB + 7, 128), f32),
+            pltpu.VMEM((PLANE, SLAB + 7, 128), f32),
             pltpu.VMEM((DEPTH, 8, EXTENT), f32),
             pltpu.VMEM((DEPTH, 8, EXTENT), f32),
             pltpu.VMEM((1, 128), f32),
             pltpu.VMEM((DEPTH, 1, 128), f32),
             pltpu.VMEM((EXTENT, 128), f32),
             pltpu.VMEM((EXTENT, 128), f32),
-            dma((4,)),
-            dma((PLANE,)), dma((PLANE,)), dma((PLANE,)), dma((PLANE,)),
+            pltpu.VMEM((128, EXTENT), bf16),
+            pltpu.VMEM((2, 128, EXTENT), bf16),
+            dma((9,)),
+            dma((PLANE,)), dma((PLANE,)),
             dma((DEPTH,)), dma((DEPTH,)), dma((DEPTH,)), dma((DEPTH,)),
             dma, dma,
             pltpu.SemaphoreType.REGULAR((3,)), pltpu.SemaphoreType.REGULAR((2,)),
         ],
         compiler_params=pltpu.CompilerParams(collective_id=0, has_side_effects=True),
         name="subtomogram_average",
-    )(orientation, wedge_index, half_set, particles[0], shell_map, first, second, back)
-    return maps, fsc[0, :NSHELL]
+    )(
+        orientation, wedge_index, half_set, particles[0], shell_map, first, second, back, spread
+    )
+    final = pltpu.with_memory_space_constraint(final, pltpu.VMEM)
+    shells = pltpu.with_memory_space_constraint(shells, pltpu.VMEM)
+    return pl.pallas_call(
+        finish,
+        out_shape=(
+            jax.ShapeDtypeStruct((2, 2, 2, 1, EXTENT), f32),
+            jax.ShapeDtypeStruct((NSHELL,), f32),
+        ),
+        in_specs=[vmem, vmem],
+        out_specs=(vmem, vmem),
+        name="hand_out",
+    )(final, shells)
 
 
 def solution(mesh):

time: 40.8 us -> 37.1 us (0.909)
  local copies, waits for them, and re-layouts: 2.48 us -> 0 us
  Pallas kernels: 35.5 us -> 34.4 us
    unnamed x1 -> x0, local copies, waits for them, and re-layouts: 1.29 us -> none
    squeeze x1 -> x0, local copies, waits for them, and re-layouts: 1.18 us -> none  [shards(): return (maps, fsc[0, :NSHELL])]
    pallas_call x1 -> x2, Pallas kernels: 35.5 us -> 34.4 us  [the longest x1 33.8 us: shards(): pl.pallas_call(body, out_shape=(pltpu.VMEM((8, EXTENT), f32), pltpu.VMEM(...]
where the time goes in v3:
time: 37.1 us; the launch traced here: 37 us
  Pallas kernels  34.4 us (93%)
  between operations  2.57 us (7%)
    pallas_call x1, Pallas kernels, shards(): pl.pallas_call(body, out_shape=(pltpu.VMEM((8, EXTENT), f32), pltpu.VMEM(...  33.8 us

profile of v3, /device:TPU:1, one launch (start us, length us, event | category | flops | bytes accessed | tf_op | source)
XLA Modules:
  0.0 37.0 jit_solution(3713419538087561621)
XLA Ops:
  2.6 33.8 %subtomogram_average.1 = (f32[8,256]{1,0:T(8,128)S(1)}, f32[8,128]{1,0:T(8,128)S(1)}) custom-call(s32[1]{0:T(128)S(6)} %copy.11.orient_t, s32[1]{0:T(128)S(6)} %copy.12.wedge_t, s32[1]{0:T(128)S(6)} %copy.13.half_t, f32[2,2,128,128]{3,2,1,0:T(8,128)} %bitcast.1, s32[2,1,256]{2,1,0:T(1,128)} %shell_t.1, bf16[2,256,256]{2,1,0:T(8,128)(2,1)} %constant.23.first_t, ...), custom_call_target="tpu_custom_call" | custom-call | tf_op jit(solution)/shard_map/subtomogram_average/pallas_call | solution.py:351
  36.4 0.6 %hand_out.1 = (f32[2,2,2,1,256]{4,3,2,1,0:T(1,128)}, f32[32]{0:T(128)}) custom-call(f32[8,256]{1,0:T(8,128)S(1)} %get-tuple-element.4.final, f32[8,128]{1,0:T(8,128)S(1)} %get-tuple-element.5.shells), custom_call_target="tpu_custom_call" | custom-call | tf_op jit(solution)/shard_map/hand_out/pallas_call | solution.py:390

commit v4 on v3

--- a/solution.py
+++ b/solution.py
@@ -25,6 +25,8 @@
 NT = (((1,), (1,)), ((), ()))
 NN = (((1,), (0,)), ((), ()))
 MAPLANE = 96
+GROUPS = (8, 8, 8, 8)
+SUMS = 17
 TAG = 2 * 2 * DEPTH
 SLAB = TAG + 1
 SIGN = 16
@@ -94,20 +96,24 @@
     orient_t, wedge_t, half_t, particle, shell_t, first_t, second_t, back_t, spread_t,
     maps_ref, fsc_ref,
     orient, wedge, half, source, shell, first, second, back, spread, slab_out, slab_in,
-    sum_out, sum_in, count_out, count_in, row_out, row_in, inside_ref, member_ref,
-    load_sem, slab_s, slab_r, sum_s, sum_r, count_s, count_r, row_s, row_r,
+    sum_out, sum_in, row_out, row_in, inside_ref, member_ref,
+    load_sem, slab_s, slab_r, sum_s, sum_r, row_s, row_r,
     above_sem, below_sem,
 ):
     px, py = lax.axis_index("px"), lax.axis_index("py")
     me = px * LINE + py
     side, level = lax.div(px, DEPTH), lax.rem(px, DEPTH)
     place = side * LINE + py
+    y = lax.div(py, 4)
+    ys = [y] + [lax.rem(y + b, 4) for b in range(1, 4)]
+    near_bit, core = lax.rem(lax.div(py, 2), 2), lax.rem(py, 2)
+    low = [near_bit * 2 + core, near_bit * 2 + 1 - core]
+    low += [2 - near_bit * 2 + core, 3 - near_bit * 2 - core]
     sides = [side, 1 - side]
-    lines = [py] + [lax.rem(py + b, LINE) for b in range(1, LINE)]
-    far_first = [8, 9, 10, 11, 7, 6, 5, 4, 12, 13, 14, 15, 3, 2, 1, 0]
-    offsets = [(a, b) for b in far_first for a in (1, 0)][:-1]
-    plane = [(sides[a], lines[b]) for a, b in offsets]
-    slots = [offsets.index((a, (LINE - b) % LINE)) for a, b in offsets]
+    offsets = [(1, 2, 1), (1, 2, 0), (0, 2, 3), (1, 1, 1), (1, 2, 3), (1, 3, 1), (0, 2, 2), (1, 1, 0), (1, 2, 2), (1, 3, 0), (0, 1, 3), (0, 2, 1), (0, 3, 3), (1, 0, 1), (1, 1, 3), (1, 3, 3), (0, 1, 2), (0, 2, 0), (0, 3, 2), (1, 0, 0), (1, 1, 2), (1, 3, 2), (0, 0, 3), (0, 1, 1), (0, 3, 1), (1, 0, 3), (0, 0, 2), (0, 1, 0), (0, 3, 0), (1, 0, 2), (0, 0, 1)]
+    bunch = [n for n, size in enumerate(GROUPS) for _ in range(size)]
+    plane = [(sides[a], ys[b] * 4 + low[c]) for a, b, c in offsets]
+    slots = [offsets.index((a, (4 - b) % 4, c)) for a, b, c in offsets]
     levels = [level] + [lax.rem(level + c, DEPTH) for c in range(1, DEPTH)]
     column = [levels[c] for c in (4, 3, 5, 2, 6, 1, 7)]
     above = (side * DEPTH + levels[1], py)
@@ -117,15 +123,13 @@
         (half_t, half), (second_t, second), (spread_t, spread), (shell_t, shell), (back_t, back),
     ]
     loads = [pltpu.make_async_copy(a, b, load_sem.at[i]) for i, (a, b) in enumerate(pairs)]
-    for load in loads[:5]:
-        load.start()
     barrier = pltpu.get_barrier_semaphore()
     for a, b in plane:
         pl.semaphore_signal(barrier, 1, device_id=(a * DEPTH + level, b), device_id_type=MESH)
     for neighbour in (above, below):
         pl.semaphore_signal(barrier, 1, device_id=neighbour, device_id_type=MESH)
 
-    for load in loads[5:]:
+    for load in loads:
         load.start()
     for load in loads[2:5]:
         load.wait()
@@ -171,16 +175,11 @@
     slab_in[PLANE - 1] = slab_out[place]
     pl.semaphore_wait(barrier, PLANE + 1)
 
-    sent = []
     for k, (a, b) in enumerate(plane):
-        sent.append(
-            pltpu.make_async_remote_copy(
-                slab_out.at[a * LINE + b, pl.ds(0, SLAB)], slab_in.at[slots[k], pl.ds(0, SLAB)],
-                slab_s.at[k], slab_r.at[slots[k]], (a * DEPTH + level, b), MESH,
-            )
-        )
-    for copy in sent:
-        copy.start()
+        pltpu.make_async_remote_copy(
+            slab_out.at[a * LINE + b, pl.ds(0, SLAB)], slab_in.at[slots[k], pl.ds(0, SLAB)],
+            slab_s, slab_r.at[bunch[slots[k]]], (a * DEPTH + level, b), MESH,
+        ).start()
     for step in range(3):
         pl.semaphore_signal(above_sem.at[step], 1, device_id=above, device_id_type=MESH)
         if step < 2:
@@ -201,11 +200,10 @@
     spread_map = spread[...]
     totals = [[jnp.zeros((DEPTH, 2 * EXTENT), f32) for z in range(2)] for h in range(2)]
     counts = jnp.zeros((1, 128), f32)
-    group = 8
-    arrivals = {slots[k]: copy for k, copy in enumerate(sent)}
-    for start in range(PLANE - group, -1, -group):
-        for k in range(start, min(start + group, PLANE - 1)):
-            arrivals[k].wait_recv()
+    for turn_in, group in enumerate(GROUPS):
+        start = sum(GROUPS[:turn_in])
+        landed = slab_in.at[pl.ds(start, min(group, PLANE - 1 - start)), pl.ds(0, SLAB)]
+        pltpu.make_async_copy(landed, landed, slab_r.at[turn_in]).wait()
         tags = slab_in[start : start + group, TAG, :]
         counts = counts + jnp.sum(tags, axis=0, keepdims=True)
         vectors = dot(tags.astype(bf16), spread_map, NN)
@@ -233,37 +231,28 @@
     for h in range(2):
         for c in range(2):
             for z in range(2):
-                sum_out[:, h * 4 + c * 2 + z, :] = totals[h][z][:, c * EXTENT : (c + 1) * EXTENT]
-    count_out[...] = counts
-    count_in[level] = counts
+                for q in range(2):
+                    base = c * EXTENT + q * 128
+                    sum_out[:, q * 8 + h * 4 + c * 2 + z, :] = totals[h][z][:, base : base + 128]
+    sum_out[:, SUMS - 1, :] = jnp.broadcast_to(counts, (DEPTH, 128))
     sum_in[level] = sum_out[level]
 
-    summed = []
-    for k, other in enumerate(column):
-        to = (side * DEPTH + other, py)
-        summed.append(
-            pltpu.make_async_remote_copy(
-                count_out, count_in.at[level], count_s.at[k], count_r.at[k], to, MESH
-            )
-        )
-        summed.append(
-            pltpu.make_async_remote_copy(
-                sum_out.at[other], sum_in.at[level], sum_s.at[k], sum_r.at[k], to, MESH
-            )
-        )
-    for copy in summed:
-        copy.start()
+    for other in column:
+        pltpu.make_async_remote_copy(
+            sum_out.at[other, pl.ds(0, SUMS)], sum_in.at[level, pl.ds(0, SUMS)],
+            sum_s, sum_r, (side * DEPTH + other, py), MESH,
+        ).start()
     comp = lax.broadcasted_iota(jnp.int32, (8, 128), 0)
     lane = lax.broadcasted_iota(jnp.int32, (8, 128), 1)
     inside = inside_ref[...]
     members = [member_ref[0], member_ref[1]]
-    for copy in summed:
-        copy.wait_recv()
-    total = sum_in[0]
-    count = count_in[0]
+    landed = sum_in.at[pl.ds(0, DEPTH - 1), pl.ds(0, SUMS)]
+    pltpu.make_async_copy(landed, landed, sum_r).wait()
+    total = sum_in[0, :SUMS]
     for k in range(1, DEPTH):
-        total = total + sum_in[k]
-        count = count + count_in[k]
+        total = total + sum_in[k, :SUMS]
+    count = total[SUMS - 1 :]
+    total = jnp.concatenate([total[:8], total[8:16]], 1)
     by_half = jnp.where(lane // 8 == comp // 4, count, 0.0)
     masked_count = dot(by_half.astype(bf16), inside, NN)
     full_count = jnp.sum(by_half, axis=1, keepdims=True)
@@ -327,8 +316,9 @@
     second_power = pltpu.roll(sums, 128 - 2 * NSHELL, 1)
     fsc_ref[...] = sums / (jnp.sqrt(first_power * second_power) + 1e-06)
 
-    for copy in sent + summed:
-        copy.wait_send()
+    gone = slab_out.at[pl.ds(0, PLANE - 1), pl.ds(0, SLAB)]
+    pltpu.make_async_copy(gone, gone, slab_s).wait()
+    pltpu.make_async_copy(landed, landed, sum_s).wait()
     pltpu.make_async_copy(whole, whole, row_s).wait()
 
 
@@ -366,18 +356,14 @@
             pltpu.VMEM((128, 2 * EXTENT), bf16),
             pltpu.VMEM((PLANE, SLAB + 7, 128), f32),
             pltpu.VMEM((PLANE, SLAB + 7, 128), f32),
-            pltpu.VMEM((DEPTH, 8, EXTENT), f32),
-            pltpu.VMEM((DEPTH, 8, EXTENT), f32),
-            pltpu.VMEM((1, 128), f32),
-            pltpu.VMEM((DEPTH, 1, 128), f32),
+            pltpu.VMEM((DEPTH, SUMS + 7, 128), f32),
+            pltpu.VMEM((DEPTH, SUMS + 7, 128), f32),
             pltpu.VMEM((EXTENT, 128), f32),
             pltpu.VMEM((EXTENT, 128), f32),
             pltpu.VMEM((128, EXTENT), bf16),
             pltpu.VMEM((2, 128, EXTENT), bf16),
             dma((9,)),
-            dma((PLANE,)), dma((PLANE,)),
-            dma((DEPTH,)), dma((DEPTH,)), dma((DEPTH,)), dma((DEPTH,)),
-            dma, dma,
+            dma, dma((len(GROUPS),)), dma, dma, dma, dma,
             pltpu.SemaphoreType.REGULAR((3,)), pltpu.SemaphoreType.REGULAR((2,)),
         ],
         compiler_params=pltpu.CompilerParams(collective_id=0, has_side_effects=True),

time: 37.1 us -> 35.8 us (0.965)
  Pallas kernels: 34.4 us -> 33.1 us
    pallas_call x1, Pallas kernels: 33.8 us -> 32.5 us  [shards(): pl.pallas_call(body, out_shape=(pltpu.VMEM((8, EXTENT), f32), pltpu.VMEM(...]
where the time goes in v4:
time: 35.8 us; the launch traced here: 35.7 us
  Pallas kernels  33.1 us (92%)
  between operations  2.57 us (7%)
    pallas_call x1, Pallas kernels, shards(): pl.pallas_call(body, out_shape=(pltpu.VMEM((8, EXTENT), f32), pltpu.VMEM(...  32.5 us

profile of v4, /device:TPU:1, one launch (start us, length us, event | category | flops | bytes accessed | tf_op | source)
XLA Modules:
  0.0 35.7 jit_solution(7189988608814566540)
XLA Ops:
  2.6 32.5 %subtomogram_average.1 = (f32[8,256]{1,0:T(8,128)S(1)}, f32[8,128]{1,0:T(8,128)S(1)}) custom-call(s32[1]{0:T(128)S(6)} %copy.11.orient_t, s32[1]{0:T(128)S(6)} %copy.12.wedge_t, s32[1]{0:T(128)S(6)} %copy.13.half_t, f32[2,2,128,128]{3,2,1,0:T(8,128)} %bitcast.1, s32[2,1,256]{2,1,0:T(1,128)} %shell_t.1, bf16[2,256,256]{2,1,0:T(8,128)(2,1)} %constant.23.first_t, ...), custom_call_target="tpu_custom_call" | custom-call | tf_op jit(solution)/shard_map/subtomogram_average/pallas_call | solution.py:341
  35.1 0.6 %hand_out.1 = (f32[2,2,2,1,256]{4,3,2,1,0:T(1,128)}, f32[32]{0:T(128)}) custom-call(f32[8,256]{1,0:T(8,128)S(1)} %get-tuple-element.4.final, f32[8,128]{1,0:T(8,128)S(1)} %get-tuple-element.5.shells), custom_call_target="tpu_custom_call" | custom-call | tf_op jit(solution)/shard_map/hand_out/pallas_call | solution.py:376

commit v5 on v4

--- a/solution.py
+++ b/solution.py
@@ -52,7 +52,7 @@
     cosine, sine = np.cos(angle) * scale, np.sin(angle) * scale
     second = np.block([[cosine, -sine], [sine, cosine]])
     angle = (freq[:, None] * freq[None, :] % EXTENT) * unit
-    back = np.concatenate([np.cos(angle), np.sin(angle)], 1) * scale
+    back = np.concatenate([np.cos(angle), np.sin(angle)], 0) * scale
     spread = np.zeros((128, 2 * EXTENT), np.float32)
     size = np.minimum(freq, EXTENT - freq)
     for kind in range(SIGN):
@@ -74,6 +74,13 @@
 
 def dot3(a, b, dims):
     return dot(a[0], b[0], dims) + (dot(a[0], b[1], dims) + dot(a[1], b[0], dims))
+
+
+def dot3_few(a, b):
+    rows = a.shape[0]
+    upper, lower = cut(a)
+    both = dot(jnp.concatenate([upper, lower], 0), b[0], NN)
+    return both[:rows] + (both[rows:] + dot(upper, b[1], NN))
 
 
 def magnitude(index):
@@ -261,28 +268,25 @@
     average = total / jnp.maximum(cover, 1.0)
 
     powers = jnp.concatenate([average * average, average * pltpu.roll(average, 4, 0)], 0)
-    powers = cut(powers)
-    p_row = lax.broadcasted_iota(jnp.int32, (16, 128), 0)
-    p_lane = lax.broadcasted_iota(jnp.int32, (16, 128), 1)
+    powers = jnp.concatenate(cut(powers), 0)
+    p_row = lax.broadcasted_iota(jnp.int32, (32, 128), 0) % 16
+    p_lane = lax.broadcasted_iota(jnp.int32, (32, 128), 1)
     wanted = jnp.where(p_row < 8, 1 + p_row // 4, jnp.where(p_row < 12, 0, 4))
-    shells = jnp.zeros((1, 128), f32)
-    for z in range(2):
-        part = dot(powers[0], members[z], NT) + dot(powers[1], members[z], NT)
-        part = jnp.where((p_row % 2 == z) & (p_lane // NSHELL == wanted), part, 0.0)
-        shells = shells + jnp.sum(part, axis=0, keepdims=True)
+    part = jnp.where(p_row % 2 == 0, dot(powers, members[0], NT), dot(powers, members[1], NT))
+    shells = jnp.sum(jnp.where(p_lane // NSHELL == wanted, part, 0.0), axis=0, keepdims=True)
 
     back_pair = (back[0], back[1])
     pair = jnp.concatenate([average, quarter_phase(average)], 1)
+    middle = dot3_few(pair, back_pair)
     padded = jnp.concatenate(
         [
-            jnp.zeros((MAPLANE, 2 * EXTENT), f32),
-            pair,
-            jnp.zeros((128 - MAPLANE - 8, 2 * EXTENT), f32),
+            jnp.zeros((MAPLANE, EXTENT), f32),
+            middle,
+            jnp.zeros((128 - MAPLANE - 8, EXTENT), f32),
         ],
         0,
     )
-    middle = dot3(back_pair, cut(padded), NT)
-    row_out[...] = middle + shells
+    row_out[...] = padded.T + shells
     row_in[pl.ds(me, 1)] = row_out[pl.ds(me, 1)]
 
     def send_row(a, c, b):
@@ -309,7 +313,7 @@
     sums = jnp.sum(rows, axis=0, keepdims=True)
     values = rows.T[MAPLANE : MAPLANE + 8]
     pair = jnp.concatenate([values, quarter_phase(values)], 1)
-    final = dot3(cut(pair), back_pair, NT)
+    final = dot3_few(pair, back_pair)
     maps_ref[...] = final
     sums = jnp.broadcast_to(sums, (8, 128))
     first_power = pltpu.roll(sums, 128 - NSHELL, 1)
@@ -352,7 +356,7 @@
             pltpu.VMEM((2, 1, EXTENT), jnp.int32),
             pltpu.VMEM((2, EXTENT, EXTENT), bf16),
             pltpu.VMEM((2, EXTENT, 2 * EXTENT), bf16),
-            pltpu.VMEM((2, EXTENT, 2 * EXTENT), bf16),
+            pltpu.VMEM((2, 2 * EXTENT, EXTENT), bf16),
             pltpu.VMEM((128, 2 * EXTENT), bf16),
             pltpu.VMEM((PLANE, SLAB + 7, 128), f32),
             pltpu.VMEM((PLANE, SLAB + 7, 128), f32),

time: 35.8 us -> 35.5 us (level)
  no operation moved by 1% of the time
where the time goes in v5:
time: 35.5 us; the launch traced here: 35.4 us
  Pallas kernels  32.8 us (92%)
  between operations  2.57 us (7%)
    pallas_call x1, Pallas kernels, shards(): pl.pallas_call(body, out_shape=(pltpu.VMEM((8, EXTENT), f32), pltpu.VMEM(...  32.2 us

profile of v5, /device:TPU:1, one launch (start us, length us, event | category | flops | bytes accessed | tf_op | source)
XLA Modules:
  0.0 35.4 jit_solution(9423136133865658219)
XLA Ops:
  2.6 32.2 %subtomogram_average.1 = (f32[8,256]{1,0:T(8,128)S(1)}, f32[8,128]{1,0:T(8,128)S(1)}) custom-call(s32[1]{0:T(128)S(6)} %copy.11.orient_t, s32[1]{0:T(128)S(6)} %copy.12.wedge_t, s32[1]{0:T(128)S(6)} %copy.13.half_t, f32[2,2,128,128]{3,2,1,0:T(8,128)} %bitcast.1, s32[2,1,256]{2,1,0:T(1,128)} %shell_t.1, bf16[2,256,256]{2,1,0:T(8,128)(2,1)} %constant.23.first_t, ...), custom_call_target="tpu_custom_call" | custom-call | tf_op jit(solution)/shard_map/subtomogram_average/pallas_call | solution.py:345
  34.8 0.6 %hand_out.1 = (f32[2,2,2,1,256]{4,3,2,1,0:T(1,128)}, f32[32]{0:T(128)}) custom-call(f32[8,256]{1,0:T(8,128)S(1)} %get-tuple-element.4.final, f32[8,128]{1,0:T(8,128)S(1)} %get-tuple-element.5.shells), custom_call_target="tpu_custom_call" | custom-call | tf_op jit(solution)/shard_map/hand_out/pallas_call | solution.py:380
